TPU v7x, 32 devices: a whole 2x2x4 slice. The times are simulated.
32 devices in a mesh: tile: 16 (over z, y, x), lev: 2 (over core).
Axes of the slice: x: 2, y: 2, z: 4, core: 2. Of those that a mesh axis runs over, the one named last changes fastest.
Arguments:
- increments: bfloat16 [136, 256, 1024], P('lev', 'tile'), may hold values from -30 to 30
- projection: bfloat16 [80, 136], replicated, may hold values from -0.5 to 0.5
- helmholtz: float32 [80], P('lev'), may hold values from 0.05 to 4
Outputs:
- solution: float32 [80, 256, 1024], P('lev', 'tile')
- residual: float32 [80, 256, 1024], P('lev', 'tile')
All inputs are finite; a program needn't handle non-finite values.
Results may differ from a plain program's by a relative error of at most 0.00075.
Values may be sent and summed in bfloat16 or wider, within the bound.
A program may use at most 192 MiB of HBM per device.

v0:
```python
import jax
import jax.numpy as jnp
import numpy as np
from jax import lax
from jax.sharding import PartitionSpec as P

S = 4
BLOCKS = 2
highest = lax.Precision.HIGHEST


def extended(block, sides, width):
    for axis, dim in sides:
        count = lax.axis_size(axis)
        forward = [(i, i + 1) for i in range(count - 1)]
        backward = [(target, source) for source, target in forward]
        low = lax.ppermute(
            lax.slice_in_dim(block, block.shape[dim] - width, None, axis=dim), axis, forward
        )
        high = lax.ppermute(lax.slice_in_dim(block, 0, width, axis=dim), axis, backward)
        block = jnp.concatenate([low, block, high], axis=dim)
    return block


def shift_matrix():
    width = 2 * S + 1
    table = np.zeros((width, width), np.float32)
    for index in range(S):
        table[index + 1, index] = 1.0
    for index in range(S - 1):
        table[S + 2 + index, S + 1 + index] = 1.0
    return jnp.asarray(table, jnp.float32)


def stencil_rows(field, weight_col):
    padded = extended(field, (("tile", 1),), 1)
    side = jnp.pad(field, ((0, 0), (0, 0), (1, 1)))
    beside_all = padded[:, 2:, :] + padded[:, :-2, :] + side[:, :, 2:] + side[:, :, :-2]
    return weight_col * beside_all


def quadratic(gram, left, right):
    return jnp.einsum("ma,mab,mb->m", left, gram, right, precision=highest)


def combine(coef, vectors):
    total = coef[:, 0, None, None] * vectors[0]
    for index in range(1, len(vectors)):
        total = total + coef[:, index, None, None] * vectors[index]
    return total


def inner_table(vectors):
    width = len(vectors)
    cached = {}
    for first in range(width):
        for second in range(first, width):
            cached[first, second] = jnp.sum(vectors[first] * vectors[second], axis=(1, 2))
    rows_list = []
    for first in range(width):
        entries = []
        for second in range(width):
            entries.append(cached[min(first, second), max(first, second)])
        rows_list.append(jnp.stack(entries, axis=1))
    return jnp.stack(rows_list, axis=1)


def shards(increments, projection, helmholtz):
    lev_count, rows_x, cells_y = increments.shape
    mode_count = projection.shape[0] // lax.axis_size("lev")
    flat = increments.reshape(lev_count, rows_x * cells_y)
    own_cols = lax.dynamic_slice_in_dim(projection, lax.axis_index("lev") * lev_count, lev_count, 1)
    modal = lax.psum_scatter(
        jnp.dot(own_cols, flat, preferred_element_type=jnp.float32),
        "lev",
        scatter_dimension=0,
        tiled=True,
    )
    modal = modal.reshape(mode_count, rows_x, cells_y)
    weight_col = (1.0 / (4.0 + helmholtz))[:, None, None]
    width = 2 * S + 1
    shifter = shift_matrix()
    solution = jnp.zeros_like(modal)
    resid = modal
    direction = modal
    for block_index in range(BLOCKS):
        vectors = [direction]
        current = direction
        for power_index in range(S):
            current = stencil_rows(current, weight_col)
            vectors.append(current)
        vectors.append(resid)
        current = resid
        for power_index in range(S - 1):
            current = stencil_rows(current, weight_col)
            vectors.append(current)
        gram = inner_table(vectors)
        gram = lax.psum(gram, "tile")
        p_coef = jnp.zeros((mode_count, width), jnp.float32).at[:, 0].set(1.0)
        r_coef = jnp.zeros((mode_count, width), jnp.float32).at[:, S + 1].set(1.0)
        x_coef = jnp.zeros((mode_count, width), jnp.float32)
        squares = quadratic(gram, r_coef, r_coef)
        for step_index in range(S):
            moved = p_coef - jnp.einsum("ab,mb->ma", shifter, p_coef, precision=highest)
            alpha = (squares / quadratic(gram, p_coef, moved))[:, None]
            x_coef = x_coef + alpha * p_coef
            r_coef = r_coef - alpha * moved
            fresh = quadratic(gram, r_coef, r_coef)
            p_coef = r_coef + (fresh / squares)[:, None] * p_coef
            squares = fresh
        solution = solution + combine(x_coef, vectors)
        resid = combine(r_coef, vectors)
        direction = combine(p_coef, vectors)
    return (solution, resid)


def solution(mesh):
    in_specs = (P("lev", "tile", None), P(), P("lev"))
    out_specs = (P("lev", "tile", None), P("lev", "tile", None))
    return jax.shard_map(shards, mesh=mesh, in_specs=in_specs, out_specs=out_specs, check_vma=False)
```

profile of v0, /device:TPU:0, one launch (start us, length us, event | category | flops | bytes accessed | tf_op | source)
XLA Modules:
  0.0 469.2 jit_solution(7739262353369601456)
XLA Ops:
  12.1 4.9 %fusion.44 = f32[80,16384]{1,0:T(8,128)} fusion(bf16[68,16384]{1,0:T(8,128)(2,1)} %bitcast.230, bf16[80,136]{0,1:T(8,128)(2,1)S(1)} %copy-done, s32[]{:T(128)S(6)} %select_n.3), kind=kOutput, calls=%fused_computation.212 | convolution fusion | flops 178257920 | bytes 7489540 | tf_op jit(solution)/shard_map/dot_general | solution.py:74
  17.0 15.9 %reduce-scatter.2.cloned.1.call-done = f32[40,16384]{1,0:T(8,128)} async-done(((f32[80,16384]{1,0:T(8,128)}), f32[40,16384]{1,0:T(8,128)}) %reduce-scatter.2.cloned.1.call-update) | async-done | bytes 2621456 | tf_op jit(solution)/shard_map/reduce_scatter | solution.py:73
  36.3 4.6 collective-permute-start.1
  52.1 5.0 %collective-permute-start.3 = (f32[40,1,1024]{2,0,1:T(8,128)S(1)}, f32[40,1,1024]{2,0,1:T(8,128)S(1)}, u32[]{:S(2)}, u32[]{:S(2)}) collective-permute-start(f32[40,1,1024]{2,0,1:T(8,128)S(1)} %get-tuple-element.129), channel_id=1, source_target_pairs={{0,2},{2,4},{4,6},{6,8},{8,10},{10,12},{12,14},{14,16},{16,18},{18... | collective-permute-start | bytes 491528 | tf_op jit(solution)/shard_map/ppermute | solution.py:17
  61.8 5.6 %fusion.5 = f32[40,16,1024]{2,0,1:T(8,128)S(1)} fusion(f32[40,16,1024]{2,0,1:T(8,128)} %copy-done.18, f32[40,1,1024]{2,0,1:T(8,128)S(1)} %collective-permute-done.3, f32[40,1,1024]{2,0,1:T(8,128)S(1)} %collective-permute-done.2, f32[40]{0:T(128)S(1)} %add_divide_fusion), kind=kLoop, calls=%fused_computation.27 | loop fusion | flops 3932160 | bytes 5570720 | tf_op jit(solution)/shard_map/mul | solution.py:39
  69.6 5.0 %collective-permute-start.5 = (f32[40,1,1024]{2,0,1:T(8,128)}, f32[40,1,1024]{2,0,1:T(8,128)S(1)}, u32[]{:S(2)}, u32[]{:S(2)}) collective-permute-start(f32[40,1,1024]{2,0,1:T(8,128)} %get-tuple-element.127), channel_id=1, source_target_pairs={{0,2},{2,4},{4,6},{6,8},{8,10},{10,12},{12,14},{14,16},{16,18},{18... | collective-permute-start | bytes 491528 | tf_op jit(solution)/shard_map/ppermute | solution.py:17
  81.8 5.5 %fusion.8 = f32[40,16,1024]{2,0,1:T(8,128)S(1)} fusion(f32[40,16,1024]{2,0,1:T(8,128)} %copy-done.6, f32[40,1,1024]{2,0,1:T(8,128)S(1)} %collective-permute-done.5, f32[40,1,1024]{2,0,1:T(8,128)S(1)} %collective-permute-done.4, f32[40]{0:T(128)S(1)} %add_divide_fusion), kind=kLoop, calls=%fused_computation.30 | loop fusion | flops 3932160 | bytes 5570720 | tf_op jit(solution)/shard_map/mul | solution.py:39
  88.9 4.9 %collective-permute-start.7 = (f32[40,1,1024]{2,0,1:T(8,128)S(1)}, f32[40,1,1024]{2,0,1:T(8,128)S(1)}, u32[]{:S(2)}, u32[]{:S(2)}) collective-permute-start(f32[40,1,1024]{2,0,1:T(8,128)S(1)} %get-tuple-element.125), channel_id=1, source_target_pairs={{0,2},{2,4},{4,6},{6,8},{8,10},{10,12},{12,14},{14,16},{16,18},{18... | collective-permute-start | bytes 491528 | tf_op jit(solution)/shard_map/ppermute | solution.py:17
  98.5 5.4 %multiply_reduce_fusion.45 = (f32[40]{0:T(128)S(1)}, f32[40]{0:T(128)S(1)}, f32[40]{0:T(128)S(1)}, f32[40]{0:T(128)S(1)}, f32[40]{0:T(128)S(1)}, /*index=5*/f32[...) fusion(f32[40,16,1024]{2,0,1:T(8,128)S(1)} %fusion.8, ...), kind=kLoop, calls=%fused_computation.138 | loop fusion | flops 26213840 | bytes 11143520 | tf_op jit(solution)/shard_map/reduce_sum | solution.py:58
  104.2 75.3 %psum.14 = f32[40,9,9]{0,2,1:T(8,128)S(1)} all-reduce(f32[40,9,9]{0,2,1:T(8,128)S(1)} %constant_dynamic-update-slice_fusion), channel_id=1, replica_groups=mesh['tile'=16,'lev'=2] {'tile'}, use_global_device_ids=true, to_apply=%region_17.18 | all-reduce | flops 3240 | bytes 25920 | tf_op jit(solution)/shard_map/psum | solution.py:98
  183.8 13.6 %multiply_add_fusion.2 = f32[40,16,1024]{2,0,1:T(8,128)S(1)} fusion(f32[40,16,1024]{2,0,1:T(8,128)} %copy-done.6, f32[40,16,1024]{2,0,1:T(8,128)} %get-tuple-element.109, f32[40]{0:T(128)S(1)} %get-tuple-element.162, f32[40]{0:T(128)S(1)} %get-tuple-element.163, f32[40]{0:T(128)S(1)} %get-tuple-element.164, f32[40]{0:T(128)S(1)} %get-tuple-element.165, ...), kind=kLoop, calls=%fused_computation.137 | loop fusion | flops 19005440 | bytes 13764160 | tf_op jit(solution)/shard_map/add | solution.py:49
  198.7 4.6 collective-permute-start.9
  203.3 5.8 %multiply_add_fusion.1 = f32[40,16,1024]{2,0,1:T(8,128)S(1)} fusion(f32[40,16,1024]{2,0,1:T(8,128)S(1)} %copy-done.7, f32[40,16,1024]{2,0,1:T(8,128)S(1)} %copy-done.17, f32[40]{0:T(128)S(1)} %get-tuple-element.171, f32[40]{0:T(128)S(1)} %get-tuple-element.172, f32[40]{0:T(128)S(1)} %get-tuple-element.173, f32[40]{0:T(128)S(1)} %get-tuple-element.174, ...), kind=kLoop, calls=%fused_computation.131 | loop fusion | flops 19005440 | bytes 13764160 | tf_op jit(solution)/shard_map/add | solution.py:49
  211.9 4.6 collective-permute-start.11
  217.8 4.6 collective-permute-start.17
  225.2 5.0 %collective-permute-start.13 = (f32[40,1,1024]{2,0,1:T(8,128)S(1)}, f32[40,1,1024]{2,0,1:T(8,128)S(1)}, u32[]{:S(2)}, u32[]{:S(2)}) collective-permute-start(f32[40,1,1024]{2,0,1:T(8,128)S(1)} %get-tuple-element.115), channel_id=1, source_target_pairs={{0,2},{2,4},{4,6},{6,8},{8,10},{10,12},{12,14},{14,16},{16,18},{18... | collective-permute-start | bytes 491528 | tf_op jit(solution)/shard_map/ppermute | solution.py:17
  239.2 6.9 %collective-permute-start.19 = (f32[40,1,1024]{2,0,1:T(8,128)S(1)}, f32[40,1,1024]{2,0,1:T(8,128)S(1)}, u32[]{:S(2)}, u32[]{:S(2)}) collective-permute-start(f32[40,1,1024]{2,0,1:T(8,128)S(1)} %get-tuple-element.121), channel_id=1, source_target_pairs={{0,2},{2,4},{4,6},{6,8},{8,10},{10,12},{12,14},{14,16},{16,18},{18... | collective-permute-start | bytes 491528 | tf_op jit(solution)/shard_map/ppermute | solution.py:17
  247.4 6.1 %collective-permute-start.15 = (f32[40,1,1024]{2,0,1:T(8,128)S(1)}, f32[40,1,1024]{2,0,1:T(8,128)}, u32[]{:S(2)}, u32[]{:S(2)}) collective-permute-start(f32[40,1,1024]{2,0,1:T(8,128)S(1)} %get-tuple-element.113), channel_id=1, source_target_pairs={{0,2},{2,4},{4,6},{6,8},{8,10},{10,12},{12,14},{14,16},{16,18},{18... | collective-permute-start | bytes 491528 | tf_op jit(solution)/shard_map/ppermute | solution.py:17
  257.8 5.7 %collective-permute-start.21 = (f32[40,1,1024]{2,0,1:T(8,128)S(1)}, f32[40,1,1024]{2,0,1:T(8,128)}, u32[]{:S(2)}, u32[]{:S(2)}) collective-permute-start(f32[40,1,1024]{2,0,1:T(8,128)S(1)} %get-tuple-element.111), channel_id=1, source_target_pairs={{0,2},{2,4},{4,6},{6,8},{8,10},{10,12},{12,14},{14,16},{16,18},{18... | collective-permute-start | bytes 491528 | tf_op jit(solution)/shard_map/ppermute | solution.py:17
  265.7 24.5 %multiply_reduce_fusion = (f32[40]{0:T(128)}, f32[40]{0:T(128)}, f32[40]{0:T(128)}, f32[40]{0:T(128)}, f32[40]{0:T(128)}, /*index=5*/f32[40]{0:T(128)}, f32[40]{...) fusion(f32[40,16,1024]{2,0,1:T(8,128)} %copy-done.20, ...), kind=kLoop, calls=%fused_computation.91 | loop fusion | flops 70777080 | bytes 21961920 | tf_op jit(solution)/shard_map/reduce_sum | solution.py:58
  308.2 77.3 %psum.15 = f32[40,9,9]{0,2,1:T(8,128)S(1)} all-reduce(f32[40,9,9]{0,2,1:T(8,128)} %constant_dynamic-update-slice_fusion.9), channel_id=1, replica_groups=mesh['tile'=16,'lev'=2] {'tile'}, use_global_device_ids=true, to_apply=%region_64.65 | all-reduce | flops 3240 | bytes 25920 | tf_op jit(solution)/shard_map/psum | solution.py:98
  422.2 19.2 %multiply_add_fusion = f32[40,16,1024]{2,0,1:T(8,128)} fusion(f32[40,16,1024]{2,0,1:T(8,128)} %get-tuple-element.108, f32[40,16,1024]{2,0,1:T(8,128)} %copy-done.15, f32[40,16,1024]{2,0,1:T(8,128)} %copy-done.11, f32[40,16,1024]{2,0,1:T(8,128)} %get-tuple-element.107, f32[40,16,1024]{2,0,1:T(8,128)} %copy-done.16, f32[40,16,1024]{2,0,1:T(8,128)} %copy-done.13, ...), kind=kLoop, calls=%fused_computation.89 | loop fusion | flops 19005440 | bytes 21628480 | tf_op jit(solution)/shard_map/add | solution.py:49
  441.5 4.9 %copy.22 = f32[40,16,1024]{2,1,0:T(8,128)} copy(f32[40,16,1024]{2,0,1:T(8,128)} %multiply_add_fusion) | data formatting | bytes 5242880
  446.5 12.8 %add_add_fusion = f32[40,16,1024]{2,0,1:T(8,128)S(1)} fusion(f32[40,16,1024]{2,0,1:T(8,128)} %get-tuple-element.108, f32[40,16,1024]{2,0,1:T(8,128)} %copy-done.15, f32[40,16,1024]{2,0,1:T(8,128)S(1)} %copy-done.12, f32[40,16,1024]{2,0,1:T(8,128)} %get-tuple-element.107, f32[40,16,1024]{2,0,1:T(8,128)} %copy-done.16, f32[40,16,1024]{2,0,1:T(8,128)S(1)} %copy-done.14, ...), kind=kLoop, calls=%fused_computation.90 | loop fusion | flops 38666240 | bytes 32771040 | tf_op jit(solution)/shard_map/add | solution.py:111
  (343 shorter events, 124.9 us)
Async XLA Ops:
  7.2 25.7 %reduce-scatter.2.cloned.1.call-start = ((), (), s32[]{:S(2)}) async-start(), calls=%async_computation.1 | async-start | bytes 7864320 | tf_op jit(solution)/shard_map/reduce_scatter | solution.py:73
  35.0 8.3 %collective-permute-start = (f32[40,1,1024]{2,0,1:T(8,128)S(1)}, f32[40,1,1024]{2,0,1:T(8,128)S(1)}, u32[]{:S(2)}, u32[]{:S(2)}) collective-permute-start(f32[40,1,1024]{2,0,1:T(8,128)S(1)} %get-tuple-element.130), channel_id=1, source_target_pairs={{2,0},{4,2},{6,4},{8,6},{10,8},{12,10},{14,12},{16,14},{18,16},{20... | collective-permute-start | bytes 491528 | tf_op jit(solution)/shard_map/ppermute | solution.py:20
  36.3 11.5 %collective-permute-start.1 = (f32[40,1,1024]{2,0,1:T(8,128)S(1)}, f32[40,1,1024]{2,0,1:T(8,128)S(1)}, u32[]{:S(2)}, u32[]{:S(2)}) collective-permute-start(f32[40,1,1024]{2,0,1:T(8,128)S(1)} %get-tuple-element.131), channel_id=1, source_target_pairs={{0,2},{2,4},{4,6},{6,8},{8,10},{10,12},{12,14},{14,16},{16,18},{18... | collective-permute-start | bytes 491528 | tf_op jit(solution)/shard_map/ppermute | solution.py:17
  40.9 142.9 %copy-start.35 = (f32[40]{0:T(128)}, f32[40]{0:T(128)S(1)}, u32[]{:S(2)}) copy-start(f32[40]{0:T(128)S(1)} %add_divide_fusion) | copy-start | bytes 484
  50.8 9.1 %collective-permute-start.2 = (f32[40,1,1024]{2,0,1:T(8,128)}, f32[40,1,1024]{2,0,1:T(8,128)S(1)}, u32[]{:S(2)}, u32[]{:S(2)}) collective-permute-start(f32[40,1,1024]{2,0,1:T(8,128)} %get-tuple-element.128), channel_id=1, source_target_pairs={{2,0},{4,2},{6,4},{8,6},{10,8},{12,10},{14,12},{16,14},{18,16},{20... | collective-permute-start | bytes 491528 | tf_op jit(solution)/shard_map/ppermute | solution.py:20
  52.1 9.7 %collective-permute-start.3 = (f32[40,1,1024]{2,0,1:T(8,128)S(1)}, f32[40,1,1024]{2,0,1:T(8,128)S(1)}, u32[]{:S(2)}, u32[]{:S(2)}) collective-permute-start(f32[40,1,1024]{2,0,1:T(8,128)S(1)} %get-tuple-element.129), channel_id=1, source_target_pairs={{0,2},{2,4},{4,6},{6,8},{8,10},{10,12},{12,14},{14,16},{16,18},{18... | collective-permute-start | bytes 491528 | tf_op jit(solution)/shard_map/ppermute | solution.py:17
  68.3 9.0 %collective-permute-start.4 = (f32[40,1,1024]{2,0,1:T(8,128)}, f32[40,1,1024]{2,0,1:T(8,128)S(1)}, u32[]{:S(2)}, u32[]{:S(2)}) collective-permute-start(f32[40,1,1024]{2,0,1:T(8,128)} %get-tuple-element.126), channel_id=1, source_target_pairs={{2,0},{4,2},{6,4},{8,6},{10,8},{12,10},{14,12},{16,14},{18,16},{20... | collective-permute-start | bytes 491528 | tf_op jit(solution)/shard_map/ppermute | solution.py:20
  69.6 12.2 %collective-permute-start.5 = (f32[40,1,1024]{2,0,1:T(8,128)}, f32[40,1,1024]{2,0,1:T(8,128)S(1)}, u32[]{:S(2)}, u32[]{:S(2)}) collective-permute-start(f32[40,1,1024]{2,0,1:T(8,128)} %get-tuple-element.127), channel_id=1, source_target_pairs={{0,2},{2,4},{4,6},{6,8},{8,10},{10,12},{12,14},{14,16},{16,18},{18... | collective-permute-start | bytes 491528 | tf_op jit(solution)/shard_map/ppermute | solution.py:17
  87.4 8.9 %collective-permute-start.6 = (f32[40,1,1024]{2,0,1:T(8,128)S(1)}, f32[40,1,1024]{2,0,1:T(8,128)S(1)}, u32[]{:S(2)}, u32[]{:S(2)}) collective-permute-start(f32[40,1,1024]{2,0,1:T(8,128)S(1)} %get-tuple-element.124), channel_id=1, source_target_pairs={{2,0},{4,2},{6,4},{8,6},{10,8},{12,10},{14,12},{16,14},{18,16},{20... | collective-permute-start | bytes 491528 | tf_op jit(solution)/shard_map/ppermute | solution.py:20
  88.9 9.6 %collective-permute-start.7 = (f32[40,1,1024]{2,0,1:T(8,128)S(1)}, f32[40,1,1024]{2,0,1:T(8,128)S(1)}, u32[]{:S(2)}, u32[]{:S(2)}) collective-permute-start(f32[40,1,1024]{2,0,1:T(8,128)S(1)} %get-tuple-element.125), channel_id=1, source_target_pairs={{0,2},{2,4},{4,6},{6,8},{8,10},{10,12},{12,14},{14,16},{16,18},{18... | collective-permute-start | bytes 491528 | tf_op jit(solution)/shard_map/ppermute | solution.py:17
  197.4 11.7 %collective-permute-start.8 = (f32[40,1,1024]{2,0,1:T(8,128)S(1)}, f32[40,1,1024]{2,0,1:T(8,128)S(1)}, u32[]{:S(2)}, u32[]{:S(2)}) collective-permute-start(f32[40,1,1024]{2,0,1:T(8,128)S(1)} %get-tuple-element.118), channel_id=1, source_target_pairs={{2,0},{4,2},{6,4},{8,6},{10,8},{12,10},{14,12},{16,14},{18,16},{20... | collective-permute-start | bytes 491528 | tf_op jit(solution)/shard_map/ppermute | solution.py:20
  198.7 10.4 %collective-permute-start.9 = (f32[40,1,1024]{2,0,1:T(8,128)S(1)}, f32[40,1,1024]{2,0,1:T(8,128)S(1)}, u32[]{:S(2)}, u32[]{:S(2)}) collective-permute-start(f32[40,1,1024]{2,0,1:T(8,128)S(1)} %get-tuple-element.119), channel_id=1, source_target_pairs={{0,2},{2,4},{4,6},{6,8},{8,10},{10,12},{12,14},{14,16},{16,18},{18... | collective-permute-start | bytes 491528 | tf_op jit(solution)/shard_map/ppermute | solution.py:17
  210.6 11.8 %collective-permute-start.10 = (f32[40,1,1024]{2,0,1:T(8,128)S(1)}, f32[40,1,1024]{2,0,1:T(8,128)S(1)}, u32[]{:S(2)}, u32[]{:S(2)}) collective-permute-start(f32[40,1,1024]{2,0,1:T(8,128)S(1)} %get-tuple-element.116), channel_id=1, source_target_pairs={{2,0},{4,2},{6,4},{8,6},{10,8},{12,10},{14,12},{16,14},{18,16},{20... | collective-permute-start | bytes 491528 | tf_op jit(solution)/shard_map/ppermute | solution.py:20
  211.9 10.5 %collective-permute-start.11 = (f32[40,1,1024]{2,0,1:T(8,128)S(1)}, f32[40,1,1024]{2,0,1:T(8,128)S(1)}, u32[]{:S(2)}, u32[]{:S(2)}) collective-permute-start(f32[40,1,1024]{2,0,1:T(8,128)S(1)} %get-tuple-element.117), channel_id=1, source_target_pairs={{0,2},{2,4},{4,6},{6,8},{8,10},{10,12},{12,14},{14,16},{16,18},{18... | collective-permute-start | bytes 491528 | tf_op jit(solution)/shard_map/ppermute | solution.py:17
  216.5 13.7 %collective-permute-start.16 = (f32[40,1,1024]{2,0,1:T(8,128)S(1)}, f32[40,1,1024]{2,0,1:T(8,128)S(1)}, u32[]{:S(2)}, u32[]{:S(2)}) collective-permute-start(f32[40,1,1024]{2,0,1:T(8,128)S(1)} %get-tuple-element.122), channel_id=1, source_target_pairs={{2,0},{4,2},{6,4},{8,6},{10,8},{12,10},{14,12},{16,14},{18,16},{20... | collective-permute-start | bytes 491528 | tf_op jit(solution)/shard_map/ppermute | solution.py:20
  217.8 12.4 %collective-permute-start.17 = (f32[40,1,1024]{2,0,1:T(8,128)S(1)}, f32[40,1,1024]{2,0,1:T(8,128)S(1)}, u32[]{:S(2)}, u32[]{:S(2)}) collective-permute-start(f32[40,1,1024]{2,0,1:T(8,128)S(1)} %get-tuple-element.123), channel_id=1, source_target_pairs={{0,2},{2,4},{4,6},{6,8},{8,10},{10,12},{12,14},{14,16},{16,18},{18... | collective-permute-start | bytes 491528 | tf_op jit(solution)/shard_map/ppermute | solution.py:17
  223.9 8.7 %collective-permute-start.12 = (f32[40,1,1024]{2,0,1:T(8,128)S(1)}, f32[40,1,1024]{2,0,1:T(8,128)S(1)}, u32[]{:S(2)}, u32[]{:S(2)}) collective-permute-start(f32[40,1,1024]{2,0,1:T(8,128)S(1)} %get-tuple-element.114), channel_id=1, source_target_pairs={{2,0},{4,2},{6,4},{8,6},{10,8},{12,10},{14,12},{16,14},{18,16},{20... | collective-permute-start | bytes 491528 | tf_op jit(solution)/shard_map/ppermute | solution.py:20
  225.2 9.3 %collective-permute-start.13 = (f32[40,1,1024]{2,0,1:T(8,128)S(1)}, f32[40,1,1024]{2,0,1:T(8,128)S(1)}, u32[]{:S(2)}, u32[]{:S(2)}) collective-permute-start(f32[40,1,1024]{2,0,1:T(8,128)S(1)} %get-tuple-element.115), channel_id=1, source_target_pairs={{0,2},{2,4},{4,6},{6,8},{8,10},{10,12},{12,14},{14,16},{16,18},{18... | collective-permute-start | bytes 491528 | tf_op jit(solution)/shard_map/ppermute | solution.py:17
  237.9 15.7 %collective-permute-start.18 = (f32[40,1,1024]{2,0,1:T(8,128)S(1)}, f32[40,1,1024]{2,0,1:T(8,128)S(1)}, u32[]{:S(2)}, u32[]{:S(2)}) collective-permute-start(f32[40,1,1024]{2,0,1:T(8,128)S(1)} %get-tuple-element.120), channel_id=1, source_target_pairs={{2,0},{4,2},{6,4},{8,6},{10,8},{12,10},{14,12},{16,14},{18,16},{20... | collective-permute-start | bytes 491528 | tf_op jit(solution)/shard_map/ppermute | solution.py:20
  239.2 14.4 %collective-permute-start.19 = (f32[40,1,1024]{2,0,1:T(8,128)S(1)}, f32[40,1,1024]{2,0,1:T(8,128)S(1)}, u32[]{:S(2)}, u32[]{:S(2)}) collective-permute-start(f32[40,1,1024]{2,0,1:T(8,128)S(1)} %get-tuple-element.121), channel_id=1, source_target_pairs={{0,2},{2,4},{4,6},{6,8},{8,10},{10,12},{12,14},{14,16},{16,18},{18... | collective-permute-start | bytes 491528 | tf_op jit(solution)/shard_map/ppermute | solution.py:17
  246.1 18.0 %collective-permute-start.14 = (f32[40,1,1024]{2,0,1:T(8,128)S(1)}, f32[40,1,1024]{2,0,1:T(8,128)}, u32[]{:S(2)}, u32[]{:S(2)}) collective-permute-start(f32[40,1,1024]{2,0,1:T(8,128)S(1)} %get-tuple-element.112), channel_id=1, source_target_pairs={{2,0},{4,2},{6,4},{8,6},{10,8},{12,10},{14,12},{16,14},{18,16},{20... | collective-permute-start | bytes 491528 | tf_op jit(solution)/shard_map/ppermute | solution.py:20
  247.4 16.7 %collective-permute-start.15 = (f32[40,1,1024]{2,0,1:T(8,128)S(1)}, f32[40,1,1024]{2,0,1:T(8,128)}, u32[]{:S(2)}, u32[]{:S(2)}) collective-permute-start(f32[40,1,1024]{2,0,1:T(8,128)S(1)} %get-tuple-element.113), channel_id=1, source_target_pairs={{0,2},{2,4},{4,6},{6,8},{8,10},{10,12},{12,14},{14,16},{16,18},{18... | collective-permute-start | bytes 491528 | tf_op jit(solution)/shard_map/ppermute | solution.py:17
  256.5 7.8 %collective-permute-start.20 = (f32[40,1,1024]{2,0,1:T(8,128)S(1)}, f32[40,1,1024]{2,0,1:T(8,128)}, u32[]{:S(2)}, u32[]{:S(2)}) collective-permute-start(f32[40,1,1024]{2,0,1:T(8,128)S(1)} %get-tuple-element.110), channel_id=1, source_target_pairs={{2,0},{4,2},{6,4},{8,6},{10,8},{12,10},{14,12},{16,14},{18,16},{20... | collective-permute-start | bytes 491528 | tf_op jit(solution)/shard_map/ppermute | solution.py:20
  257.8 7.9 %collective-permute-start.21 = (f32[40,1,1024]{2,0,1:T(8,128)S(1)}, f32[40,1,1024]{2,0,1:T(8,128)}, u32[]{:S(2)}, u32[]{:S(2)}) collective-permute-start(f32[40,1,1024]{2,0,1:T(8,128)S(1)} %get-tuple-element.111), channel_id=1, source_target_pairs={{0,2},{2,4},{4,6},{6,8},{8,10},{10,12},{12,14},{14,16},{16,18},{18... | collective-permute-start | bytes 491528 | tf_op jit(solution)/shard_map/ppermute | solution.py:17
  (72 other events, 1497.5 us)
Sparse Core Ops, SparseCore 0:
  17.1 15.7 reduce-scatter.1
where the time goes:
time: 471 us; the launch traced here: 469 us
  blocking collectives  153 us (32%)
  other arithmetic  124 us (26%)
  starting transfers between devices  71.4 us (15%)
  local copies, waits for them, and re-layouts  55.5 us (12%)
  waiting for transfers between devices  41.9 us (9%)
  between operations  16.7 us (4%)
  matrix products  7.1 us (2%)
    psum x2, blocking collectives, shards(): gram = lax.psum(gram, 'tile')  153 us
    ppermute x11, starting transfers between devices, extended(): lax.ppermute(lax.slice_in_dim(block, block.shape[dim] - width, None, axis...  56.9 us
    add x3, other arithmetic, combine(): total = total + coef[:, index, None, None] * vectors[index]  38.5 us
    reduce_sum x3, other arithmetic, inner_table(): jnp.sum(vectors[first] * vectors[second], axis=(1, 2))  30.2 us
    unnamed x180, local copies, waits for them, and re-layouts  29.2 us
    mul x7, other arithmetic, stencil_rows(): return weight_col * beside_all  20.1 us
    ppermute x11, waiting for transfers between devices, extended(): lax.ppermute(lax.slice_in_dim(block, block.shape[dim] - width, None, axis...  16.6 us
    reduce_scatter x1, waiting for transfers between devices, shards(): lax.psum_scatter(jnp.dot(own_cols, flat, preferred_element_type=jnp.float...  15.9 us
  transfers between devices with their start and end apart: 23, of which 12 were waited for; matrix products, arithmetic and copies ran while one was open for 2% of the time, Pallas kernels for 0%

commit v1 on v0

--- a/solution.py
+++ b/solution.py
@@ -95,7 +95,9 @@
             current = stencil_rows(current, weight_col)
             vectors.append(current)
         gram = inner_table(vectors)
-        gram = lax.psum(gram, "tile")
+        gram = gram
+        for hop in (1, 2, 4, 8):
+            gram = gram + lax.ppermute(gram, "tile", [(dev, dev ^ hop) for dev in range(16)])
         p_coef = jnp.zeros((mode_count, width), jnp.float32).at[:, 0].set(1.0)
         r_coef = jnp.zeros((mode_count, width), jnp.float32).at[:, S + 1].set(1.0)
         x_coef = jnp.zeros((mode_count, width), jnp.float32)

time: 471 us -> 352 us (0.75)
  blocking collectives: 153 us -> 0 us
  starting transfers between devices: 71.4 us -> 102 us
  waiting for transfers between devices: 41.9 us -> 58.6 us
  other arithmetic: 124 us -> 117 us
  local copies, waits for them, and re-layouts: 55.5 us -> 49 us
    psum x2 -> x0, blocking collectives: 153 us -> none  [shards(): gram = lax.psum(gram, 'tile')]
    ppermute x0 -> x8, starting transfers between devices: none -> 29.4 us  [shards(): lax.ppermute(gram, 'tile', [(dev, dev ^ hop) for dev in range(16)])]
    ppermute x0 -> x8, waiting for transfers between devices: none -> 14.6 us  [shards(): lax.ppermute(gram, 'tile', [(dev, dev ^ hop) for dev in range(16)])]
    mul x7, other arithmetic: 20.1 us -> 11.8 us  [stencil_rows(): return weight_col * beside_all]
    unnamed x180 -> x162, local copies, waits for them, and re-layouts: 29.2 us -> 23.1 us
  transfers between devices with their start and end apart: 23 -> 31, of which waited for: 12 -> 22; matrix products, arithmetic and copies ran while one was open for 2% -> 3% of each run, Pallas kernels for 0% -> 0%
where the time goes in v1:
time: 352 us; the launch traced here: 350 us
  other arithmetic  117 us (33%)
  starting transfers between devices  102 us (29%)
  waiting for transfers between devices  58.6 us (17%)
  local copies, waits for them, and re-layouts  49 us (14%)
  between operations  16.7 us (5%)
  matrix products  7.1 us (2%)
    ppermute x11, starting transfers between devices, extended(): lax.ppermute(lax.slice_in_dim(block, block.shape[dim] - width, None, axis...  58.3 us
    add x3, other arithmetic, combine(): total = total + coef[:, index, None, None] * vectors[index]  37.6 us
    reduce_sum x3, other arithmetic, inner_table(): jnp.sum(vectors[first] * vectors[second], axis=(1, 2))  30.4 us
    ppermute x8, starting transfers between devices, shards(): lax.ppermute(gram, 'tile', [(dev, dev ^ hop) for dev in range(16)])  29.4 us
    unnamed x162, local copies, waits for them, and re-layouts  23.1 us
    ppermute x11, waiting for transfers between devices, extended(): lax.ppermute(lax.slice_in_dim(block, block.shape[dim] - width, None, axis...  16.7 us
    reduce_scatter x1, waiting for transfers between devices, shards(): lax.psum_scatter(jnp.dot(own_cols, flat, preferred_element_type=jnp.float...  15.9 us
    ppermute x8, waiting for transfers between devices, shards(): lax.ppermute(gram, 'tile', [(dev, dev ^ hop) for dev in range(16)])  14.6 us
  transfers between devices with their start and end apart: 31, of which 22 were waited for; matrix products, arithmetic and copies ran while one was open for 3% of the time, Pallas kernels for 0%

profile of v1, /device:TPU:0, one launch (start us, length us, event | category | flops | bytes accessed | tf_op | source)
XLA Modules:
  0.0 349.9 jit_solution(12589210711471095633)
XLA Ops:
  12.1 4.9 %fusion.44 = f32[80,16384]{1,0:T(8,128)} fusion(bf16[68,16384]{1,0:T(8,128)(2,1)} %bitcast.230, bf16[80,136]{0,1:T(8,128)(2,1)S(1)} %copy-done, s32[]{:T(128)S(6)} %select_n.3), kind=kOutput, calls=%fused_computation.212 | convolution fusion | flops 178257920 | bytes 7489540 | tf_op jit(solution)/shard_map/dot_general | solution.py:74
  17.0 15.9 %reduce-scatter.2.cloned.1.call-done = f32[40,16384]{1,0:T(8,128)} async-done(((f32[80,16384]{1,0:T(8,128)}), f32[40,16384]{1,0:T(8,128)}) %reduce-scatter.2.cloned.1.call-update) | async-done | bytes 2621456 | tf_op jit(solution)/shard_map/reduce_scatter | solution.py:73
  36.3 4.6 %collective-permute-start.1 = (f32[40,1,1024]{2,0,1:T(8,128)S(1)}, f32[40,1,1024]{2,0,1:T(8,128)S(1)}, u32[]{:S(2)}, u32[]{:S(2)}) collective-permute-start(f32[40,1,1024]{2,0,1:T(8,128)S(1)} %get-tuple-element.133), channel_id=1, source_target_pairs={{0,2},{2,4},{4,6},{6,8},{8,10},{10,12},{12,14},{14,16},{16,18},{18... | collective-permute-start | bytes 491528 | tf_op jit(solution)/shard_map/ppermute | solution.py:17
  43.3 4.5 %collective-permute-done.1 = f32[40,1,1024]{2,0,1:T(8,128)S(1)} collective-permute-done((f32[40,1,1024]{2,0,1:T(8,128)S(1)}, f32[40,1,1024]{2,0,1:T(8,128)S(1)}, u32[]{:S(2)}, u32[]{:S(2)}) %collective-permute-start.1) | collective-permute-done | bytes 163872 | tf_op jit(solution)/shard_map/ppermute | solution.py:17
  50.6 5.0 %collective-permute-start.3 = (f32[40,1,1024]{2,0,1:T(8,128)S(1)}, f32[40,1,1024]{2,0,1:T(8,128)S(1)}, u32[]{:S(2)}, u32[]{:S(2)}) collective-permute-start(f32[40,1,1024]{2,0,1:T(8,128)S(1)} %get-tuple-element.131), channel_id=1, source_target_pairs={{0,2},{2,4},{4,6},{6,8},{8,10},{10,12},{12,14},{14,16},{16,18},{18... | collective-permute-start | bytes 491528 | tf_op jit(solution)/shard_map/ppermute | solution.py:17
  62.9 5.3 %collective-permute-start.5 = (f32[40,1,1024]{2,0,1:T(8,128)S(1)}, f32[40,1,1024]{2,0,1:T(8,128)S(1)}, u32[]{:S(2)}, u32[]{:S(2)}) collective-permute-start(f32[40,1,1024]{2,0,1:T(8,128)S(1)} %get-tuple-element.129), channel_id=1, source_target_pairs={{0,2},{2,4},{4,6},{6,8},{8,10},{10,12},{12,14},{14,16},{16,18},{18... | collective-permute-start | bytes 491528 | tf_op jit(solution)/shard_map/ppermute | solution.py:17
  77.6 5.2 %collective-permute-start.7 = (f32[40,1,1024]{2,0,1:T(8,128)S(1)}, f32[40,1,1024]{2,0,1:T(8,128)S(1)}, u32[]{:S(2)}, u32[]{:S(2)}) collective-permute-start(f32[40,1,1024]{2,0,1:T(8,128)S(1)} %get-tuple-element.127), channel_id=1, source_target_pairs={{0,2},{2,4},{4,6},{6,8},{8,10},{10,12},{12,14},{14,16},{16,18},{18... | collective-permute-start | bytes 491528 | tf_op jit(solution)/shard_map/ppermute | solution.py:17
  87.5 5.4 %multiply_reduce_fusion.45 = (f32[40]{0:T(128)S(1)}, f32[40]{0:T(128)S(1)}, f32[40]{0:T(128)S(1)}, f32[40]{0:T(128)S(1)}, f32[40]{0:T(128)S(1)}, /*index=5*/f32[...) fusion(f32[40,16,1024]{2,0,1:T(8,128)S(1)} %fusion.8, ...), kind=kLoop, calls=%fused_computation.138 | loop fusion | flops 26213840 | bytes 11143520 | tf_op jit(solution)/shard_map/reduce_sum | solution.py:58
  118.8 13.7 %multiply_add_fusion.2 = f32[40,16,1024]{2,0,1:T(8,128)S(1)} fusion(f32[40,16,1024]{2,0,1:T(8,128)} %copy-done.6, f32[40,16,1024]{2,0,1:T(8,128)} %get-tuple-element.111, f32[40]{0:T(128)S(1)} %get-tuple-element.164, f32[40]{0:T(128)S(1)} %get-tuple-element.165, f32[40]{0:T(128)S(1)} %get-tuple-element.166, f32[40]{0:T(128)S(1)} %get-tuple-element.167, ...), kind=kLoop, calls=%fused_computation.137 | loop fusion | flops 19005440 | bytes 13764160 | tf_op jit(solution)/shard_map/add | solution.py:49
  133.8 4.6 %collective-permute-start.13 = (f32[40,1,1024]{2,0,1:T(8,128)S(1)}, f32[40,1,1024]{2,0,1:T(8,128)S(1)}, u32[]{:S(2)}, u32[]{:S(2)}) collective-permute-start(f32[40,1,1024]{2,0,1:T(8,128)S(1)} %get-tuple-element.121), channel_id=1, source_target_pairs={{0,2},{2,4},{4,6},{6,8},{8,10},{10,12},{12,14},{14,16},{16,18},{18... | collective-permute-start | bytes 491528 | tf_op jit(solution)/shard_map/ppermute | solution.py:17
  138.4 4.8 %multiply_add_fusion.1 = f32[40,16,1024]{2,0,1:T(8,128)S(1)} fusion(f32[40,16,1024]{2,0,1:T(8,128)S(1)} %copy-done.7, f32[40,16,1024]{2,0,1:T(8,128)S(1)} %copy-done.17, f32[40]{0:T(128)S(1)} %get-tuple-element.173, f32[40]{0:T(128)S(1)} %get-tuple-element.174, f32[40]{0:T(128)S(1)} %get-tuple-element.175, f32[40]{0:T(128)S(1)} %get-tuple-element.176, ...), kind=kLoop, calls=%fused_computation.131 | loop fusion | flops 19005440 | bytes 13764160 | tf_op jit(solution)/shard_map/add | solution.py:49
  146.0 4.7 %collective-permute-start.15 = (f32[40,1,1024]{2,0,1:T(8,128)S(1)}, f32[40,1,1024]{2,0,1:T(8,128)S(1)}, u32[]{:S(2)}, u32[]{:S(2)}) collective-permute-start(f32[40,1,1024]{2,0,1:T(8,128)S(1)} %get-tuple-element.119), channel_id=1, source_target_pairs={{0,2},{2,4},{4,6},{6,8},{8,10},{10,12},{12,14},{14,16},{16,18},{18... | collective-permute-start | bytes 491528 | tf_op jit(solution)/shard_map/ppermute | solution.py:17
  152.0 5.4 %collective-permute-start.21 = (f32[40,1,1024]{2,0,1:T(8,128)S(1)}, f32[40,1,1024]{2,0,1:T(8,128)S(1)}, u32[]{:S(2)}, u32[]{:S(2)}) collective-permute-start(f32[40,1,1024]{2,0,1:T(8,128)S(1)} %get-tuple-element.125), channel_id=1, source_target_pairs={{0,2},{2,4},{4,6},{6,8},{8,10},{10,12},{12,14},{14,16},{16,18},{18... | collective-permute-start | bytes 491528 | tf_op jit(solution)/shard_map/ppermute | solution.py:17
  160.9 5.0 %collective-permute-start.17 = (f32[40,1,1024]{2,0,1:T(8,128)S(1)}, f32[40,1,1024]{2,0,1:T(8,128)S(1)}, u32[]{:S(2)}, u32[]{:S(2)}) collective-permute-start(f32[40,1,1024]{2,0,1:T(8,128)S(1)} %get-tuple-element.117), channel_id=1, source_target_pairs={{0,2},{2,4},{4,6},{6,8},{8,10},{10,12},{12,14},{14,16},{16,18},{18... | collective-permute-start | bytes 491528 | tf_op jit(solution)/shard_map/ppermute | solution.py:17
  173.4 5.5 %collective-permute-start.23 = (f32[40,1,1024]{2,0,1:T(8,128)S(1)}, f32[40,1,1024]{2,0,1:T(8,128)S(1)}, u32[]{:S(2)}, u32[]{:S(2)}) collective-permute-start(f32[40,1,1024]{2,0,1:T(8,128)S(1)} %get-tuple-element.123), channel_id=1, source_target_pairs={{0,2},{2,4},{4,6},{6,8},{8,10},{10,12},{12,14},{14,16},{16,18},{18... | collective-permute-start | bytes 491528 | tf_op jit(solution)/shard_map/ppermute | solution.py:17
  180.1 6.6 %collective-permute-start.19 = (f32[40,1,1024]{2,0,1:T(8,128)S(1)}, f32[40,1,1024]{2,0,1:T(8,128)}, u32[]{:S(2)}, u32[]{:S(2)}) collective-permute-start(f32[40,1,1024]{2,0,1:T(8,128)S(1)} %get-tuple-element.115), channel_id=1, source_target_pairs={{0,2},{2,4},{4,6},{6,8},{8,10},{10,12},{12,14},{14,16},{16,18},{18... | collective-permute-start | bytes 491528 | tf_op jit(solution)/shard_map/ppermute | solution.py:17
  191.0 6.4 %collective-permute-start.25 = (f32[40,1,1024]{2,0,1:T(8,128)S(1)}, f32[40,1,1024]{2,0,1:T(8,128)}, u32[]{:S(2)}, u32[]{:S(2)}) collective-permute-start(f32[40,1,1024]{2,0,1:T(8,128)S(1)} %get-tuple-element.113), channel_id=1, source_target_pairs={{0,2},{2,4},{4,6},{6,8},{8,10},{10,12},{12,14},{14,16},{16,18},{18... | collective-permute-start | bytes 491528 | tf_op jit(solution)/shard_map/ppermute | solution.py:17
  199.6 24.7 %multiply_reduce_fusion = (f32[40]{0:T(128)}, f32[40]{0:T(128)}, f32[40]{0:T(128)}, f32[40]{0:T(128)}, f32[40]{0:T(128)}, /*index=5*/f32[40]{0:T(128)}, f32[40]{...) fusion(f32[40,16,1024]{2,0,1:T(8,128)} %copy-done.18, ...), kind=kLoop, calls=%fused_computation.91 | loop fusion | flops 70777080 | bytes 21961920 | tf_op jit(solution)/shard_map/reduce_sum | solution.py:58
  236.9 4.4 %collective-permute-start.26 = (f32[40,9,9]{0,2,1:T(8,128)S(1)}, f32[40,9,9]{0,2,1:T(8,128)S(1)}, u32[]{:S(2)}, u32[]{:S(2)}) collective-permute-start(f32[40,9,9]{0,2,1:T(8,128)S(1)} %constant_dynamic-update-slice_fusion.9), channel_id=1, source_target_pairs={{0,2},{2,0},{4,6},{6,4},{8,10},{10,8},{12,14},{14,12},{16,18},{18,... | collective-permute-start | bytes 38888 | tf_op jit(solution)/shard_map/ppermute | solution.py:100
  243.7 6.2 %collective-permute-start.27 = (f32[40,9,9]{0,2,1:T(8,128)S(1)}, f32[40,9,9]{0,2,1:T(8,128)S(1)}, u32[]{:S(2)}, u32[]{:S(2)}) collective-permute-start(f32[40,9,9]{0,2,1:T(8,128)S(1)} %add.408), channel_id=1, source_target_pairs={{0,4},{2,6},{4,0},{6,2},{8,12},{10,14},{12,8},{14,10},{16,20},{18,... | collective-permute-start | bytes 38888 | tf_op jit(solution)/shard_map/ppermute | solution.py:100
  252.3 5.6 %collective-permute-start.28 = (f32[40,9,9]{0,2,1:T(8,128)S(1)}, f32[40,9,9]{0,2,1:T(8,128)S(1)}, u32[]{:S(2)}, u32[]{:S(2)}) collective-permute-start(f32[40,9,9]{0,2,1:T(8,128)S(1)} %add.409), channel_id=1, source_target_pairs={{0,8},{2,10},{4,12},{6,14},{8,0},{10,2},{12,4},{14,6},{16,24},{18,... | collective-permute-start | bytes 38888 | tf_op jit(solution)/shard_map/ppermute | solution.py:100
  303.0 19.2 %multiply_add_fusion = f32[40,16,1024]{2,0,1:T(8,128)} fusion(f32[40,16,1024]{2,0,1:T(8,128)} %get-tuple-element.109, f32[40,16,1024]{2,0,1:T(8,128)} %copy-done.15, f32[40,16,1024]{2,0,1:T(8,128)} %copy-done.11, f32[40,16,1024]{2,0,1:T(8,128)} %get-tuple-element.108, f32[40,16,1024]{2,0,1:T(8,128)} %copy-done.16, f32[40,16,1024]{2,0,1:T(8,128)} %copy-done.13, ...), kind=kLoop, calls=%fused_computation.89 | loop fusion | flops 19005440 | bytes 21628480 | tf_op jit(solution)/shard_map/add | solution.py:49
  322.3 4.9 %copy.22 = f32[40,16,1024]{2,1,0:T(8,128)} copy(f32[40,16,1024]{2,0,1:T(8,128)} %multiply_add_fusion) | data formatting | bytes 5242880
  327.3 12.7 %add_add_fusion = f32[40,16,1024]{2,0,1:T(8,128)S(1)} fusion(f32[40,16,1024]{2,0,1:T(8,128)} %get-tuple-element.109, f32[40,16,1024]{2,0,1:T(8,128)} %copy-done.15, f32[40,16,1024]{2,0,1:T(8,128)S(1)} %copy-done.12, f32[40,16,1024]{2,0,1:T(8,128)} %get-tuple-element.108, f32[40,16,1024]{2,0,1:T(8,128)} %copy-done.16, f32[40,16,1024]{2,0,1:T(8,128)S(1)} %copy-done.14, ...), kind=kLoop, calls=%fused_computation.90 | loop fusion | flops 38666240 | bytes 32771040 | tf_op jit(solution)/shard_map/add | solution.py:113
  (345 shorter events, 148.0 us)
Async XLA Ops:
  7.2 25.7 %reduce-scatter.2.cloned.1.call-start = ((), (), s32[]{:S(2)}) async-start(), calls=%async_computation.1 | async-start | bytes 7864320 | tf_op jit(solution)/shard_map/reduce_scatter | solution.py:73
  35.0 8.3 %collective-permute-start = (f32[40,1,1024]{2,0,1:T(8,128)S(1)}, f32[40,1,1024]{2,0,1:T(8,128)S(1)}, u32[]{:S(2)}, u32[]{:S(2)}) collective-permute-start(f32[40,1,1024]{2,0,1:T(8,128)S(1)} %get-tuple-element.132), channel_id=1, source_target_pairs={{2,0},{4,2},{6,4},{8,6},{10,8},{12,10},{14,12},{16,14},{18,16},{20... | collective-permute-start | bytes 491528 | tf_op jit(solution)/shard_map/ppermute | solution.py:20
  36.3 11.5 %collective-permute-start.1 = (f32[40,1,1024]{2,0,1:T(8,128)S(1)}, f32[40,1,1024]{2,0,1:T(8,128)S(1)}, u32[]{:S(2)}, u32[]{:S(2)}) collective-permute-start(f32[40,1,1024]{2,0,1:T(8,128)S(1)} %get-tuple-element.133), channel_id=1, source_target_pairs={{0,2},{2,4},{4,6},{6,8},{8,10},{10,12},{12,14},{14,16},{16,18},{18... | collective-permute-start | bytes 491528 | tf_op jit(solution)/shard_map/ppermute | solution.py:17
  49.3 8.8 %collective-permute-start.2 = (f32[40,1,1024]{2,0,1:T(8,128)S(1)}, f32[40,1,1024]{2,0,1:T(8,128)S(1)}, u32[]{:S(2)}, u32[]{:S(2)}) collective-permute-start(f32[40,1,1024]{2,0,1:T(8,128)S(1)} %get-tuple-element.130), channel_id=1, source_target_pairs={{2,0},{4,2},{6,4},{8,6},{10,8},{12,10},{14,12},{16,14},{18,16},{20... | collective-permute-start | bytes 491528 | tf_op jit(solution)/shard_map/ppermute | solution.py:20
  50.6 9.5 %collective-permute-start.3 = (f32[40,1,1024]{2,0,1:T(8,128)S(1)}, f32[40,1,1024]{2,0,1:T(8,128)S(1)}, u32[]{:S(2)}, u32[]{:S(2)}) collective-permute-start(f32[40,1,1024]{2,0,1:T(8,128)S(1)} %get-tuple-element.131), channel_id=1, source_target_pairs={{0,2},{2,4},{4,6},{6,8},{8,10},{10,12},{12,14},{14,16},{16,18},{18... | collective-permute-start | bytes 491528 | tf_op jit(solution)/shard_map/ppermute | solution.py:17
  61.6 8.8 %collective-permute-start.4 = (f32[40,1,1024]{2,0,1:T(8,128)S(1)}, f32[40,1,1024]{2,0,1:T(8,128)S(1)}, u32[]{:S(2)}, u32[]{:S(2)}) collective-permute-start(f32[40,1,1024]{2,0,1:T(8,128)S(1)} %get-tuple-element.128), channel_id=1, source_target_pairs={{2,0},{4,2},{6,4},{8,6},{10,8},{12,10},{14,12},{16,14},{18,16},{20... | collective-permute-start | bytes 491528 | tf_op jit(solution)/shard_map/ppermute | solution.py:20
  62.9 11.9 %collective-permute-start.5 = (f32[40,1,1024]{2,0,1:T(8,128)S(1)}, f32[40,1,1024]{2,0,1:T(8,128)S(1)}, u32[]{:S(2)}, u32[]{:S(2)}) collective-permute-start(f32[40,1,1024]{2,0,1:T(8,128)S(1)} %get-tuple-element.129), channel_id=1, source_target_pairs={{0,2},{2,4},{4,6},{6,8},{8,10},{10,12},{12,14},{14,16},{16,18},{18... | collective-permute-start | bytes 491528 | tf_op jit(solution)/shard_map/ppermute | solution.py:17
  76.3 8.8 %collective-permute-start.6 = (f32[40,1,1024]{2,0,1:T(8,128)S(1)}, f32[40,1,1024]{2,0,1:T(8,128)S(1)}, u32[]{:S(2)}, u32[]{:S(2)}) collective-permute-start(f32[40,1,1024]{2,0,1:T(8,128)S(1)} %get-tuple-element.126), channel_id=1, source_target_pairs={{2,0},{4,2},{6,4},{8,6},{10,8},{12,10},{14,12},{16,14},{18,16},{20... | collective-permute-start | bytes 491528 | tf_op jit(solution)/shard_map/ppermute | solution.py:20
  77.6 10.0 %collective-permute-start.7 = (f32[40,1,1024]{2,0,1:T(8,128)S(1)}, f32[40,1,1024]{2,0,1:T(8,128)S(1)}, u32[]{:S(2)}, u32[]{:S(2)}) collective-permute-start(f32[40,1,1024]{2,0,1:T(8,128)S(1)} %get-tuple-element.127), channel_id=1, source_target_pairs={{0,2},{2,4},{4,6},{6,8},{8,10},{10,12},{12,14},{14,16},{16,18},{18... | collective-permute-start | bytes 491528 | tf_op jit(solution)/shard_map/ppermute | solution.py:17
  132.5 10.7 %collective-permute-start.12 = (f32[40,1,1024]{2,0,1:T(8,128)S(1)}, f32[40,1,1024]{2,0,1:T(8,128)S(1)}, u32[]{:S(2)}, u32[]{:S(2)}) collective-permute-start(f32[40,1,1024]{2,0,1:T(8,128)S(1)} %get-tuple-element.120), channel_id=1, source_target_pairs={{2,0},{4,2},{6,4},{8,6},{10,8},{12,10},{14,12},{16,14},{18,16},{20... | collective-permute-start | bytes 491528 | tf_op jit(solution)/shard_map/ppermute | solution.py:20
  133.8 9.4 %collective-permute-start.13 = (f32[40,1,1024]{2,0,1:T(8,128)S(1)}, f32[40,1,1024]{2,0,1:T(8,128)S(1)}, u32[]{:S(2)}, u32[]{:S(2)}) collective-permute-start(f32[40,1,1024]{2,0,1:T(8,128)S(1)} %get-tuple-element.121), channel_id=1, source_target_pairs={{0,2},{2,4},{4,6},{6,8},{8,10},{10,12},{12,14},{14,16},{16,18},{18... | collective-permute-start | bytes 491528 | tf_op jit(solution)/shard_map/ppermute | solution.py:17
  144.7 12.8 %collective-permute-start.14 = (f32[40,1,1024]{2,0,1:T(8,128)S(1)}, f32[40,1,1024]{2,0,1:T(8,128)S(1)}, u32[]{:S(2)}, u32[]{:S(2)}) collective-permute-start(f32[40,1,1024]{2,0,1:T(8,128)S(1)} %get-tuple-element.118), channel_id=1, source_target_pairs={{2,0},{4,2},{6,4},{8,6},{10,8},{12,10},{14,12},{16,14},{18,16},{20... | collective-permute-start | bytes 491528 | tf_op jit(solution)/shard_map/ppermute | solution.py:20
  146.0 12.1 %collective-permute-start.15 = (f32[40,1,1024]{2,0,1:T(8,128)S(1)}, f32[40,1,1024]{2,0,1:T(8,128)S(1)}, u32[]{:S(2)}, u32[]{:S(2)}) collective-permute-start(f32[40,1,1024]{2,0,1:T(8,128)S(1)} %get-tuple-element.119), channel_id=1, source_target_pairs={{0,2},{2,4},{4,6},{6,8},{8,10},{10,12},{12,14},{14,16},{16,18},{18... | collective-permute-start | bytes 491528 | tf_op jit(solution)/shard_map/ppermute | solution.py:17
  150.7 15.2 %collective-permute-start.20 = (f32[40,1,1024]{2,0,1:T(8,128)S(1)}, f32[40,1,1024]{2,0,1:T(8,128)S(1)}, u32[]{:S(2)}, u32[]{:S(2)}) collective-permute-start(f32[40,1,1024]{2,0,1:T(8,128)S(1)} %get-tuple-element.124), channel_id=1, source_target_pairs={{2,0},{4,2},{6,4},{8,6},{10,8},{12,10},{14,12},{16,14},{18,16},{20... | collective-permute-start | bytes 491528 | tf_op jit(solution)/shard_map/ppermute | solution.py:20
  152.0 13.9 %collective-permute-start.21 = (f32[40,1,1024]{2,0,1:T(8,128)S(1)}, f32[40,1,1024]{2,0,1:T(8,128)S(1)}, u32[]{:S(2)}, u32[]{:S(2)}) collective-permute-start(f32[40,1,1024]{2,0,1:T(8,128)S(1)} %get-tuple-element.125), channel_id=1, source_target_pairs={{0,2},{2,4},{4,6},{6,8},{8,10},{10,12},{12,14},{14,16},{16,18},{18... | collective-permute-start | bytes 491528 | tf_op jit(solution)/shard_map/ppermute | solution.py:17
  159.6 7.9 %collective-permute-start.16 = (f32[40,1,1024]{2,0,1:T(8,128)S(1)}, f32[40,1,1024]{2,0,1:T(8,128)S(1)}, u32[]{:S(2)}, u32[]{:S(2)}) collective-permute-start(f32[40,1,1024]{2,0,1:T(8,128)S(1)} %get-tuple-element.116), channel_id=1, source_target_pairs={{2,0},{4,2},{6,4},{8,6},{10,8},{12,10},{14,12},{16,14},{18,16},{20... | collective-permute-start | bytes 491528 | tf_op jit(solution)/shard_map/ppermute | solution.py:20
  172.1 14.7 %collective-permute-start.22 = (f32[40,1,1024]{2,0,1:T(8,128)S(1)}, f32[40,1,1024]{2,0,1:T(8,128)S(1)}, u32[]{:S(2)}, u32[]{:S(2)}) collective-permute-start(f32[40,1,1024]{2,0,1:T(8,128)S(1)} %get-tuple-element.122), channel_id=1, source_target_pairs={{2,0},{4,2},{6,4},{8,6},{10,8},{12,10},{14,12},{16,14},{18,16},{20... | collective-permute-start | bytes 491528 | tf_op jit(solution)/shard_map/ppermute | solution.py:20
  173.4 13.4 %collective-permute-start.23 = (f32[40,1,1024]{2,0,1:T(8,128)S(1)}, f32[40,1,1024]{2,0,1:T(8,128)S(1)}, u32[]{:S(2)}, u32[]{:S(2)}) collective-permute-start(f32[40,1,1024]{2,0,1:T(8,128)S(1)} %get-tuple-element.123), channel_id=1, source_target_pairs={{0,2},{2,4},{4,6},{6,8},{8,10},{10,12},{12,14},{14,16},{16,18},{18... | collective-permute-start | bytes 491528 | tf_op jit(solution)/shard_map/ppermute | solution.py:17
  178.8 18.6 %collective-permute-start.18 = (f32[40,1,1024]{2,0,1:T(8,128)S(1)}, f32[40,1,1024]{2,0,1:T(8,128)}, u32[]{:S(2)}, u32[]{:S(2)}) collective-permute-start(f32[40,1,1024]{2,0,1:T(8,128)S(1)} %get-tuple-element.114), channel_id=1, source_target_pairs={{2,0},{4,2},{6,4},{8,6},{10,8},{12,10},{14,12},{16,14},{18,16},{20... | collective-permute-start | bytes 491528 | tf_op jit(solution)/shard_map/ppermute | solution.py:20
  180.1 17.3 %collective-permute-start.19 = (f32[40,1,1024]{2,0,1:T(8,128)S(1)}, f32[40,1,1024]{2,0,1:T(8,128)}, u32[]{:S(2)}, u32[]{:S(2)}) collective-permute-start(f32[40,1,1024]{2,0,1:T(8,128)S(1)} %get-tuple-element.115), channel_id=1, source_target_pairs={{0,2},{2,4},{4,6},{6,8},{8,10},{10,12},{12,14},{14,16},{16,18},{18... | collective-permute-start | bytes 491528 | tf_op jit(solution)/shard_map/ppermute | solution.py:17
  189.7 8.5 %collective-permute-start.24 = (f32[40,1,1024]{2,0,1:T(8,128)S(1)}, f32[40,1,1024]{2,0,1:T(8,128)}, u32[]{:S(2)}, u32[]{:S(2)}) collective-permute-start(f32[40,1,1024]{2,0,1:T(8,128)S(1)} %get-tuple-element.112), channel_id=1, source_target_pairs={{2,0},{4,2},{6,4},{8,6},{10,8},{12,10},{14,12},{16,14},{18,16},{20... | collective-permute-start | bytes 491528 | tf_op jit(solution)/shard_map/ppermute | solution.py:20
  191.0 8.6 %collective-permute-start.25 = (f32[40,1,1024]{2,0,1:T(8,128)S(1)}, f32[40,1,1024]{2,0,1:T(8,128)}, u32[]{:S(2)}, u32[]{:S(2)}) collective-permute-start(f32[40,1,1024]{2,0,1:T(8,128)S(1)} %get-tuple-element.113), channel_id=1, source_target_pairs={{0,2},{2,4},{4,6},{6,8},{8,10},{10,12},{12,14},{14,16},{16,18},{18... | collective-permute-start | bytes 491528 | tf_op jit(solution)/shard_map/ppermute | solution.py:17
  243.7 8.6 %collective-permute-start.27 = (f32[40,9,9]{0,2,1:T(8,128)S(1)}, f32[40,9,9]{0,2,1:T(8,128)S(1)}, u32[]{:S(2)}, u32[]{:S(2)}) collective-permute-start(f32[40,9,9]{0,2,1:T(8,128)S(1)} %add.408), channel_id=1, source_target_pairs={{0,4},{2,6},{4,0},{6,2},{8,12},{10,14},{12,8},{14,10},{16,20},{18,... | collective-permute-start | bytes 38888 | tf_op jit(solution)/shard_map/ppermute | solution.py:100
  252.3 7.9 %collective-permute-start.28 = (f32[40,9,9]{0,2,1:T(8,128)S(1)}, f32[40,9,9]{0,2,1:T(8,128)S(1)}, u32[]{:S(2)}, u32[]{:S(2)}) collective-permute-start(f32[40,9,9]{0,2,1:T(8,128)S(1)} %add.409), channel_id=1, source_target_pairs={{0,8},{2,10},{4,12},{6,14},{8,0},{10,2},{12,4},{14,6},{16,24},{18,... | collective-permute-start | bytes 38888 | tf_op jit(solution)/shard_map/ppermute | solution.py:100
  (71 other events, 922.6 us)
Sparse Core Ops, SparseCore 0:
  17.1 15.7 reduce-scatter.1
